TPU v7x, 32 devices: a whole 2x2x4 slice. The times are simulated.
32 devices in a mesh: groups: 2 (over x), elem: 16 (over z, y, core).
Axes of the slice: x: 2, y: 2, z: 4, core: 2. Of those that a mesh axis runs over, the one named last changes fastest.
Arguments:
- snapshots: float32 [2, 4096, 16384], P(None, ('groups', 'elem')), parts along dimension 1, may hold values from -6 to 6
- delays: float32 [384, 2048], replicated, may hold values from -3 to 3
- element_order: int32 [4096], P('groups'), parts along dimension 0, may hold values from 0 to 2047, each once
- beam_table: int32 [512], P('groups'), parts along dimension 0, may hold values from 0 to 383
- band_len: int32 [8], replicated, may hold values from 1 to 4, 16 in all
Outputs:
- beams: float32 [16384, 2, 512], P('elem', None, 'groups'), parts along dimension 2
- power_db: float32 [8, 512], P(None, 'groups'), parts along dimension 1
There are 2 independent parts, one for each index of `groups`. A program takes and returns all parts, laid end to end along the dimension named above; an argument that names none is the same for every part. Nothing has to cross between parts.
Inputs may be any that keep to these rules, and one draw needn't show every extreme that they name: `element_order`: each of 0 to 2047 appears once. `band_len`: the entries sum to 16.
All inputs are finite; a program needn't handle non-finite values.
Results may differ from a plain program's by a relative error of at most 0.0003.
Values sent between devices are 32-bit elements; how exact they have to be, the bound alone decides.
A program may use at most 128 MiB of HBM per device.

v0:
```python
import math
import jax
import jax.numpy as jnp
from jax import lax
from jax.sharding import PartitionSpec as P

epsilon = 1e-06


def band_of(band_len, position, unit_count):
    band_ends = jnp.cumsum(band_len)
    band_index = jnp.sum((band_ends <= position).astype(jnp.int32))
    selector = jnp.arange(band_len.shape[0], dtype=jnp.int32) == band_index
    band_size = jnp.sum(jnp.where(selector, band_len, 0))
    band_start = jnp.sum(jnp.where(selector, band_ends, 0)) - band_size
    frequency = (band_start.astype(jnp.float32) + 0.5 * band_size.astype(jnp.float32)) / float(
        unit_count
    )
    return (frequency, band_size, selector.astype(jnp.float32))


def steering(delays, element_order, beam_table, frequency):
    delay_rows = jnp.take(delays, beam_table, axis=0)
    delay_rows = jnp.take(delay_rows, element_order, axis=1)
    phases = 2.0 * math.pi * frequency * delay_rows
    scaling = float(delays.shape[1]) ** (-0.5)
    cosines = jnp.cos(phases) * scaling
    sines = -jnp.sin(phases) * scaling
    upper_rows = jnp.concatenate([cosines.T, sines.T], axis=1)
    lower_rows = jnp.concatenate([-sines.T, cosines.T], axis=1)
    return jnp.concatenate([upper_rows, lower_rows], axis=0)


def project(arrived, weights):
    columns = arrived.shape[2]
    stacked = arrived.reshape(2 * arrived.shape[1], columns)
    return lax.dot_general(
        stacked,
        weights,
        (((0,), (0,)), ((), ())),
        precision=lax.Precision.HIGHEST,
        preferred_element_type=jnp.float32,
    )


def local(snapshots, delays, element_order, beam_table, band_len):
    unit_count = lax.axis_size("elem")
    position = lax.axis_index("elem")
    frequency, band_size, selector = band_of(band_len, position, unit_count)
    weights = steering(delays, element_order, beam_table, frequency)
    beam_count = beam_table.shape[0]
    local_elems = snapshots.shape[1]
    unit_cols = snapshots.shape[2] // unit_count
    divided = snapshots.reshape(2, local_elems, unit_count, unit_cols)
    pieces = lax.all_to_all(divided, "elem", split_axis=2, concat_axis=1, tiled=True)
    formed = project(pieces.reshape(2, pieces.shape[1], pieces.shape[3]), weights)
    column_count = formed.shape[0]
    squares = jnp.sum(formed * formed, axis=0)
    power_mean = (squares[:beam_count] + squares[beam_count:]) / (
        band_size.astype(jnp.float32) * column_count
    )
    partial_value = selector[:, None] * power_mean[None, :]
    summed = lax.psum(partial_value, "elem")
    decibels = 10.0 * jnp.log10(summed + epsilon)
    return (formed.reshape(column_count, 2, beam_count), decibels)


def solution(mesh):
    return jax.shard_map(
        local,
        mesh=mesh,
        in_specs=(P(None, ("groups", "elem"), None), P(), P("groups"), P("groups"), P()),
        out_specs=(P("elem", None, "groups"), P(None, "groups")),
        check_vma=False,
    )
```

profile of v0, /device:TPU:0, one launch (start us, length us, event | category | flops | bytes accessed | tf_op | source)
XLA Modules:
  0.0 488.5 jit_solution(5320041055812886282)
XLA Ops:
  0.6 0.0 copy-start
  0.6 17.6 %copy.16 = f32[2,128,16384]{1,2,0:T(8,128)} copy(f32[2,128,16384]{2,1,0:T(8,128)} %param.5) | data formatting | bytes 33554432 | tf_op args[0]
  18.2 11.3 %copy.17 = f32[2,128,16,1024]{1,3,0,2:T(8,128)} copy(f32[2,128,16,1024]{1,3,2,0:T(8,128)} %bitcast.19) | data formatting | bytes 33554432 | tf_op jit(solution)/shard_map/reshape | solution.py:54
  29.5 0.0 copy-start.3
  29.5 7.6 %all-to-all-start = ((f32[2,128,16,1024]{1,3,0,2:T(8,128)}), f32[2,128,16,1024]{1,3,0,2:T(8,128)}, u32[]{:S(2)}, u32[]{:S(2)}) async-start(f32[2,128,16,1024]{1,3,0,2:T(8,128)} %copy.17), calls=%async_computation | async-start | bytes 33554432 | tf_op jit(solution)/shard_map/all_to_all | solution.py:55
  37.1 0.0 copy-done.3
  37.2 0.0 copy-done
  37.2 2.7 gather_fusion
  39.9 3.1 broadcast_select_fusion
  43.0 0.0 copy-start.4
  43.0 0.0 copy-start.2
  43.0 1.9 copy.15
  44.9 0.0 copy-done.4
  44.9 0.2 reduce-window.9
  45.1 0.6 fusion.10
  45.8 1.3 fusion.11
  49.1 0.0 copy-done.2
  49.1 8.6 %gather_fusion.1 = f32[2048,256]{1,0:T(8,128)} fusion(f32[256,2048]{0,1:T(8,128)S(1)} %copy.15, s32[2048]{0:T(1024)S(1)} %fusion.9), kind=kCustom, calls=%fused_computation.1 | custom fusion | bytes 4202496 | tf_op jit(solution)/shard_map/jit(_take)/gather | solution.py:24
  57.7 0.6 fusion.12
  58.4 10.9 %fusion.14 = (f32[2048,256]{1,0:T(8,128)S(1)}, f32[2048,256]{1,0:T(8,128)}, f32[2048,256]{1,0:T(8,128)}) fusion(f32[2048,256]{1,0:T(8,128)} %gather_fusion.1, pred[2048]{0:T(1024)(128)(4,1)S(1)} %compare_and_fusion, f32[]{:T(128)S(6)} %mul_shard_map.7), kind=kLoop, calls=%fused_computation.33 | loop fusion | flops 3145728 | bytes 8390660 | tf_op jit(solution)/shard_map/neg | solution.py:30
  69.3 264.4 %all-to-all-done = f32[2,128,16,1024]{1,3,0,2:T(8,128)} async-done(((f32[2,128,16,1024]{1,3,0,2:T(8,128)}), f32[2,128,16,1024]{1,3,0,2:T(8,128)}, u32[]{:S(2)}, u32[]{:S(2)}) %all-to-all-start) | async-done | bytes 16777248 | tf_op jit(solution)/shard_map/all_to_all | solution.py:55
  333.8 18.0 %copy.18 = f32[2,128,16,1024]{3,1,2,0:T(8,128)} copy(f32[2,128,16,1024]{1,3,0,2:T(8,128)} %all-to-all-done) | data formatting | bytes 33554432 | tf_op jit(solution)/shard_map/all_to_all | solution.py:55
  351.8 33.0 %fusion.8 = (f32[512]{0:T(512)S(1)}, f32[512,1024]{1,0:T(8,128)}) fusion(f32[4096,1024]{1,0:T(8,128)} %bitcast.20, f32[2048,256]{1,0:T(8,128)} %get-tuple-element.12, f32[2048,256]{1,0:T(8,128)S(1)} %get-tuple-element.10, f32[2048,256]{1,0:T(8,128)} %get-tuple-element.11), kind=kOutput, calls=%fused_computation.11 | convolution fusion | flops 25777143808 | bytes 25167872 | tf_op jit(solution)/shard_map/dot_general | solution.py:37
  384.7 0.0 copy-start.1
  384.7 4.3 copy.19
  389.0 0.1 broadcast_multiply_fusion
  389.1 98.8 %psum.7 = f32[8,256]{1,0:T(8,128)S(1)} all-reduce(f32[8,256]{1,0:T(8,128)S(1)} %broadcast_multiply_fusion), channel_id=1, replica_groups=mesh['groups'=2,'elem'=16] {'elem'}, use_global_device_ids=true, to_apply=%region_5.6 | all-reduce | flops 2048 | bytes 16384 | tf_op jit(solution)/shard_map/psum | solution.py:63
  487.9 0.6 log_multiply_fusion
  488.5 0.0 copy-done.1
  (6 shorter events, 0.0 us)
Async XLA Ops:
  0.6 36.5 %copy-start = (f32[384,2048]{1,0:T(8,128)S(1)}, f32[384,2048]{1,0:T(8,128)}, u32[]{:S(2)}) copy-start(f32[384,2048]{1,0:T(8,128)} %param.6) | copy-start | bytes 9437188
  29.5 7.6 %copy-start.3 = (s32[256]{0:T(256)S(1)}, s32[256]{0:T(256)}, u32[]{:S(2)}) copy-start(s32[256]{0:T(256)} %param.8) | copy-start | bytes 3076
  29.5 304.2 %all-to-all-start = ((f32[2,128,16,1024]{1,3,0,2:T(8,128)}), f32[2,128,16,1024]{1,3,0,2:T(8,128)}, u32[]{:S(2)}, u32[]{:S(2)}) async-start(f32[2,128,16,1024]{1,3,0,2:T(8,128)} %copy.17), calls=%async_computation | async-start | bytes 33554432 | tf_op jit(solution)/shard_map/all_to_all | solution.py:55
  43.0 2.0 copy-start.4
  43.0 6.1 %copy-start.2 = (s32[2048]{0:T(1024)S(1)}, s32[2048]{0:T(1024)}, u32[]{:S(2)}) copy-start(s32[2048]{0:T(1024)} %param.7) | copy-start | bytes 24580
  384.7 103.8 %copy-start.1 = (f32[384,2048]{1,0:T(8,128)S(1)}, f32[384,2048]{1,0:T(8,128)}, u32[]{:S(2)}) copy-start(f32[384,2048]{1,0:T(8,128)} %param.6) | copy-start | bytes 9437188
where the time goes:
time: 489 us; the launch traced here: 488 us
  waiting for transfers between devices  264 us (54%)
  blocking collectives  98.8 us (20%)
  local copies, waits for them, and re-layouts  64.4 us (13%)
  matrix products  33 us (7%)
  other arithmetic  17.6 us (4%)
  starting transfers between devices  7.6 us (2%)
    all_to_all x1, waiting for transfers between devices, local(): lax.all_to_all(divided, 'elem', split_axis=2, concat_axis=1, tiled=True)  264 us
    psum x1, blocking collectives, local(): summed = lax.psum(partial_value, 'elem')  98.8 us
    dot_general x1, matrix products, project(): lax.dot_general(stacked, weights, (((0,), (0,)), ((), ())), precision=lax...  33 us
    unnamed x12, local copies, waits for them, and re-layouts  21.9 us
    all_to_all x1, local copies, waits for them, and re-layouts, local(): lax.all_to_all(divided, 'elem', split_axis=2, concat_axis=1, tiled=True)  18 us
    reshape x1, local copies, waits for them, and re-layouts, local(): divided = snapshots.reshape(2, local_elems, unit_count, unit_cols)  11.3 us
    neg x1, other arithmetic, steering(): lower_rows = jnp.concatenate([-sines.T, cosines.T], axis=1)  10.9 us
  transfers between devices with their start and end apart: 1, of which 1 were waited for; matrix products, arithmetic and copies ran while one was open for 6% of the time, Pallas kernels for 0%

commit v1 on v0

--- a/solution.py
+++ b/solution.py
@@ -52,7 +52,10 @@
     local_elems = snapshots.shape[1]
     unit_cols = snapshots.shape[2] // unit_count
     divided = snapshots.reshape(2, local_elems, unit_count, unit_cols)
-    pieces = lax.all_to_all(divided, "elem", split_axis=2, concat_axis=1, tiled=True)
+    peers = lax.axis_size("elem")
+    tiles = jnp.stack(jnp.split(divided, peers, axis=2), axis=0)
+    tiles = lax.all_to_all(tiles, "elem", split_axis=0, concat_axis=0)
+    pieces = jnp.concatenate(tiles, axis=1)
     formed = project(pieces.reshape(2, pieces.shape[1], pieces.shape[3]), weights)
     column_count = formed.shape[0]
     squares = jnp.sum(formed * formed, axis=0)

time: 489 us -> 507 us (1.037)
  local copies, waits for them, and re-layouts: 64.4 us -> 83.8 us
    unnamed x12 -> x27, local copies, waits for them, and re-layouts: 21.9 us -> 49 us
    all_to_all x1 -> x0, local copies, waits for them, and re-layouts: 18 us -> none  [local(): lax.all_to_all(divided, 'elem', split_axis=2, concat_axis=1, tiled=True)]
    reshape x1, local copies, waits for them, and re-layouts: 11.3 us -> 18 us  [local(): pieces = jnp.concatenate(tiles, axis=1)]
where the time goes in v1:
time: 507 us; the launch traced here: 506 us
  waiting for transfers between devices  262 us (52%)
  blocking collectives  98.8 us (19%)
  local copies, waits for them, and re-layouts  83.8 us (17%)
  matrix products  33.2 us (7%)
  other arithmetic  17.7 us (3%)
  starting transfers between devices  7.6 us (1%)
    all_to_all x1, waiting for transfers between devices, local(): tiles = lax.all_to_all(tiles, 'elem', split_axis=0, concat_axis=0)  262 us
    psum x1, blocking collectives, local(): summed = lax.psum(partial_value, 'elem')  98.8 us
    unnamed x27, local copies, waits for them, and re-layouts  49 us
    dot_general x1, matrix products, project(): lax.dot_general(stacked, weights, (((0,), (0,)), ((), ())), precision=lax...  33.2 us
    reshape x1, local copies, waits for them, and re-layouts, local(): pieces = jnp.concatenate(tiles, axis=1)  18 us
    neg x1, other arithmetic, steering(): lower_rows = jnp.concatenate([-sines.T, cosines.T], axis=1)  11.1 us
    gather x1, local copies, waits for them, and re-layouts, steering(): delay_rows = jnp.take(delay_rows, element_order, axis=1)  10.2 us
  transfers between devices with their start and end apart: 1, of which 1 were waited for; matrix products, arithmetic and copies ran while one was open for 6% of the time, Pallas kernels for 0%

profile of v1, /device:TPU:0, one launch (start us, length us, event | category | flops | bytes accessed | tf_op | source)
XLA Modules:
  0.0 505.7 jit_solution(16571479017267385593)
XLA Ops:
  0.6 0.0 copy-start
  0.6 17.6 %copy.26 = f32[2,128,16384]{1,2,0:T(8,128)} copy(f32[2,128,16384]{2,1,0:T(8,128)} %param.5) | data formatting | bytes 33554432 | tf_op args[0]
  18.2 0.0 copy-start.1
  18.2 2.4 fusion.23
  20.6 3.1 fusion.22
  23.7 2.9 fusion.21
  26.6 2.3 fusion.20
  28.9 2.3 fusion.19
  31.2 2.3 fusion.18
  33.5 2.3 fusion.17
  35.8 2.3 fusion.16
  38.1 0.0 copy-done.1
  38.1 1.1 fusion.15
  39.2 1.0 fusion.14
  40.2 1.0 fusion.13
  41.3 1.0 fusion.12
  42.3 1.1 fusion.11
  43.4 1.0 fusion.10
  44.5 1.0 fusion.9
  45.5 1.1 fusion.8
  46.6 0.0 copy-start.4
  46.6 0.0 copy-start.3
  46.6 7.6 %all-to-all-start = ((f32[16,2,128,1,1024]{2,4,1,3,0:T(8,128)}), f32[16,2,128,1,1024]{2,4,1,3,0:T(8,128)}, u32[]{:S(2)}, u32[]{:S(2)}) async-start(f32[16,2,128,1,1024]{2,4,1,3,0:T(8,128)} %fusion.8), calls=%async_computation | async-start | bytes 33554432 | tf_op jit(solution)/shard_map/all_to_all | solution.py:57
  54.2 0.0 copy-start.2
  54.2 0.0 copy-done.4
  54.2 0.2 reduce-window.9
  54.4 0.6 fusion.25
  55.0 1.3 fusion.26
  58.4 0.0 copy-done.3
  58.4 0.0 copy-done
  58.4 2.7 gather_fusion
  61.1 3.1 broadcast_select_fusion
  64.2 2.9 copy.43
  67.1 0.0 copy-done.2
  67.2 10.2 %gather_fusion.1 = f32[2048,256]{1,0:T(8,128)} fusion(f32[256,2048]{0,1:T(8,128)} %copy.43, s32[2048]{0:T(1024)S(1)} %fusion.24), kind=kCustom, calls=%fused_computation.1 | custom fusion | bytes 4202496 | tf_op jit(solution)/shard_map/jit(_take)/gather | solution.py:24
  77.3 0.6 fusion.27
  78.0 11.1 %fusion.29 = (f32[2048,256]{1,0:T(8,128)}, f32[2048,256]{1,0:T(8,128)}, f32[2048,256]{1,0:T(8,128)}) fusion(f32[2048,256]{1,0:T(8,128)} %gather_fusion.1, pred[2048]{0:T(1024)(128)(4,1)S(1)} %compare_and_fusion, f32[]{:T(128)S(6)} %mul_shard_map.7), kind=kLoop, calls=%fused_computation.64 | loop fusion | flops 3145728 | bytes 8390660 | tf_op jit(solution)/shard_map/neg | solution.py:30
  89.1 261.7 %all-to-all-done = f32[16,2,128,1,1024]{2,4,1,3,0:T(8,128)} async-done(((f32[16,2,128,1,1024]{2,4,1,3,0:T(8,128)}), f32[16,2,128,1,1024]{2,4,1,3,0:T(8,128)}, u32[]{:S(2)}, u32[]{:S(2)}) %all-to-all-start) | async-done | bytes 16777248 | tf_op jit(solution)/shard_map/all_to_all | solution.py:57
  350.8 18.0 %copy.42 = f32[2,16,128,1,1024]{4,2,1,0,3:T(8,128)} copy(f32[2,16,128,1,1024]{2,4,0,3,1:T(8,128)} %bitcast.17) | data formatting | bytes 33554432 | tf_op jit(solution)/shard_map/reshape | solution.py:58
  368.8 33.2 %multiply_reduce_fusion = (f32[512]{0:T(512)S(1)}, f32[1024,512]{0,1:T(8,128)}) fusion(f32[4096,1024]{1,0:T(8,128)} %bitcast.121, f32[2048,256]{1,0:T(8,128)} %get-tuple-element.10, f32[2048,256]{1,0:T(8,128)} %get-tuple-element.8, f32[2048,256]{1,0:T(8,128)} %get-tuple-element.9), kind=kOutput, calls=%fused_computation.13 | convolution fusion | flops 25777143808 | bytes 25167872 | tf_op jit(solution)/shard_map/dot_general | solution.py:37
  402.1 4.1 copy.44
  406.2 0.1 broadcast_multiply_fusion
  406.3 98.8 %psum.7 = f32[8,256]{1,0:T(8,128)S(1)} all-reduce(f32[8,256]{1,0:T(8,128)S(1)} %broadcast_multiply_fusion), channel_id=1, replica_groups=mesh['groups'=2,'elem'=16] {'elem'}, use_global_device_ids=true, to_apply=%region_5.6 | all-reduce | flops 2048 | bytes 16384 | tf_op jit(solution)/shard_map/psum | solution.py:66
  505.1 0.6 log_multiply_fusion
  (6 shorter events, 0.0 us)
Async XLA Ops:
  0.6 57.8 %copy-start = (f32[384,2048]{1,0:T(8,128)S(1)}, f32[384,2048]{1,0:T(8,128)}, u32[]{:S(2)}) copy-start(f32[384,2048]{1,0:T(8,128)} %param.6) | copy-start | bytes 9437188
  18.2 19.9 %copy-start.1 = (f32[2,128,16384]{1,2,0:T(8,128)S(1)}, f32[2,128,16384]{1,2,0:T(8,128)}, u32[]{:S(2)}) copy-start(f32[2,128,16384]{1,2,0:T(8,128)} %copy.26) | copy-start | bytes 50331652
  46.6 7.6 %copy-start.4 = (s32[8]{0:T(128)S(1)}, s32[8]{0:T(128)}, u32[]{:S(2)}) copy-start(s32[8]{0:T(128)} %param.9) | copy-start | bytes 100
  46.6 11.8 %copy-start.3 = (s32[256]{0:T(256)S(1)}, s32[256]{0:T(256)}, u32[]{:S(2)}) copy-start(s32[256]{0:T(256)} %param.8) | copy-start | bytes 3076
  46.6 304.2 %all-to-all-start = ((f32[16,2,128,1,1024]{2,4,1,3,0:T(8,128)}), f32[16,2,128,1,1024]{2,4,1,3,0:T(8,128)}, u32[]{:S(2)}, u32[]{:S(2)}) async-start(f32[16,2,128,1,1024]{2,4,1,3,0:T(8,128)} %fusion.8), calls=%async_computation | async-start | bytes 33554432 | tf_op jit(solution)/shard_map/all_to_all | solution.py:57
  54.2 12.9 %copy-start.2 = (s32[2048]{0:T(1024)S(1)}, s32[2048]{0:T(1024)}, u32[]{:S(2)}) copy-start(s32[2048]{0:T(1024)} %param.7) | copy-start | bytes 24580
